TPU v7x, 256 devices: a whole 4x4x8 slice. The times are simulated.
256 devices in a mesh: seq: 32 (over y_lo, z, core), batch: 8 (over x, y_hi).
Axes of the slice: x: 4, y: 4 (y_hi: 2, y_lo: 2; y = y_hi * 2 + y_lo), z: 8, core: 2. Of those that a mesh axis runs over, the one named last changes fastest.
Arguments:
- embedded: bfloat16 [32768, 1024], P(('batch', 'seq')), parts along dimension 0, may hold values from -6 to 6
- w_qkv: bfloat16 [2, 1024, 3072], P(None, 'seq'), may hold values from -0.1875 to 0.1875
- w_out: bfloat16 [2, 1024, 1024], P(None, 'seq'), may hold values from -0.1875 to 0.1875
- w_pos: bfloat16 [2, 1024, 1024], P(None, None, 'seq'), may hold values from -0.1875 to 0.1875
- bias_content: float32 [2, 1024], replicated, may hold values from -3 to 3
- bias_position: float32 [2, 1024], replicated, may hold values from -3 to 3
- norm_gain: float32 [2, 1024], replicated, may hold values from 0.5 to 1.5
- norm_offset: float32 [2, 1024], replicated, may hold values from -2 to 2
- table: bfloat16 [12288, 1024], P('seq'), may hold values from -1 to 1
- targets: int32 [32768], P('batch'), parts along dimension 0, may hold values from 0 to 12287
- valid_length: int32 [8], P('batch'), parts along dimension 0, may hold values from 3969 to 4096
Outputs:
- hidden_out: bfloat16 [32768, 1024], P(('batch', 'seq')), parts along dimension 0
- token_loss: float32 [32768], P(('batch', 'seq')), parts along dimension 0
- loss_value: float32 [8], P('batch'), parts along dimension 0
There are 8 independent parts, one for each index of `batch`. A program takes and returns all parts, laid end to end along the dimension named above; an argument that names none is the same for every part. Nothing has to cross between parts.
All inputs are finite; a program needn't handle non-finite values.
Results may differ from a plain program's by a relative error of at most 0.006.
Values may be sent and summed in bfloat16 or wider, within the bound.
A program may use at most 64 MiB of HBM per device.

v0:
```python
import jax
import jax.numpy as jnp
from jax import lax
from jax.sharding import PartitionSpec as P

HEADS = 16
LAYERS = 2
norm_eps = 1e-05


def passed_along(x, axis, by):
    devices = lax.axis_size(axis)
    pairs = [(i, i + by) for i in range(devices) if 0 <= i + by < devices]
    return lax.ppermute(x, axis, pairs)


def copy_for_each(x, axis):
    devices = lax.axis_size(axis)
    return lax.all_to_all(jnp.broadcast_to(x[None], (devices, *x.shape)), axis, 0, 0, tiled=True)


def in_order(tiles, dim):
    tiles = jnp.moveaxis(tiles, 0, dim)
    dims = tiles.shape
    return tiles.reshape(*dims[:dim], dims[dim] * dims[dim + 1], *dims[dim + 2 :])


def gather_directly(x, axis, dim):
    tiles = copy_for_each(x, axis)
    return in_order(tiles, dim)


def of_everyone(x, axis):
    return copy_for_each(x, axis).astype(jnp.float32).sum(axis=0)


def sinusoid(row_count, model_width):
    distance = jnp.arange(row_count - 1, -1, -1).astype(jnp.float32)
    inverse = 1.0 / 10000.0 ** (jnp.arange(0, model_width, 2).astype(jnp.float32) / model_width)
    angles = distance[:, None] * inverse[None, :]
    return jnp.concatenate([jnp.sin(angles), jnp.cos(angles)], axis=1).astype(jnp.bfloat16)


def rel_shift(scores):
    leading = scores.shape[:-2]
    row_count, col_count = (scores.shape[-2], scores.shape[-1])
    padded = jnp.pad(scores, [(0, 0)] * len(leading) + [(0, 0), (1, 0)])
    flattened = padded.reshape(leading + (row_count * (col_count + 1),))[..., row_count:]
    return flattened.reshape(leading + (row_count, col_count))


def layer_norm(values, gain_row, offset_row):
    row_mean = jnp.mean(values, -1, keepdims=True)
    centred = values - row_mean
    spread = jnp.mean(centred * centred, -1, keepdims=True)
    return centred * lax.rsqrt(spread + norm_eps) * gain_row + offset_row


def attention_layer(
    hidden,
    qkv_shard,
    out_shard,
    pos_shard,
    content_bias,
    position_bias,
    gain_row,
    offset_row,
    pos_table,
    allowed,
):
    block_len, model_width = hidden.shape
    head_size = model_width // HEADS
    memory = passed_along(hidden, "seq", 1)
    piece_rows = lax.all_gather(qkv_shard, "seq", axis=0, tiled=True)
    own_cols = hidden
    own_part = jnp.dot(own_cols, piece_rows, preferred_element_type=jnp.float32)
    memory_part = jnp.dot(memory, piece_rows[:, model_width:], preferred_element_type=jnp.float32)
    folded = (own_part, memory_part)
    mixed_rows = folded[0]
    key_rows = mixed_rows[:, model_width : 2 * model_width].astype(jnp.bfloat16)
    value_rows = mixed_rows[:, 2 * model_width :].astype(jnp.bfloat16)
    memory_keys = folded[1][:, :model_width].astype(jnp.bfloat16)
    memory_values = folded[1][:, model_width:].astype(jnp.bfloat16)
    pos_share = jnp.dot(pos_table, pos_shard, preferred_element_type=jnp.float32).astype(
        jnp.bfloat16
    )
    pos_keys = gather_directly(pos_share, "seq", 1)
    query_rows = mixed_rows[:, :model_width]
    q_content = (
        (query_rows + content_bias).astype(jnp.bfloat16).reshape(block_len, HEADS, head_size)
    )
    q_position = (
        (query_rows + position_bias).astype(jnp.bfloat16).reshape(block_len, HEADS, head_size)
    )
    keys_all = jnp.concatenate([memory_keys, key_rows], 0).reshape(2 * block_len, HEADS, head_size)
    values_all = jnp.concatenate([memory_values, value_rows], 0).reshape(
        2 * block_len, HEADS, head_size
    )
    content = jnp.einsum("qhd,khd->hqk", q_content, keys_all, preferred_element_type=jnp.float32)
    position = rel_shift(
        jnp.einsum(
            "qhd,khd->hqk",
            q_position,
            pos_keys.reshape(2 * block_len, HEADS, head_size),
            preferred_element_type=jnp.float32,
        )
    )
    scores = (content + position) * head_size ** (-0.5)
    exp_scores = jnp.where(allowed[None], jnp.exp(scores), 0.0)
    attn_probs = (exp_scores / jnp.sum(exp_scores, -1, keepdims=True)).astype(jnp.bfloat16)
    attended = jnp.einsum(
        "hqk,khd->qhd", attn_probs, values_all, preferred_element_type=jnp.float32
    )
    attended = attended.astype(jnp.bfloat16).reshape(block_len, model_width)
    own_cols = attended
    projected = jnp.dot(
        own_cols, gather_directly(out_shard, "seq", 0), preferred_element_type=jnp.float32
    )
    return layer_norm(hidden.astype(jnp.float32) + projected, gain_row, offset_row).astype(
        jnp.bfloat16
    )


def on_device(
    embedded,
    w_qkv,
    w_out,
    w_pos,
    bias_content,
    bias_position,
    norm_gain,
    norm_offset,
    table,
    targets,
    valid_length,
):
    block_len, model_width = embedded.shape
    device_idx = lax.axis_index("seq")
    pos_table = sinusoid(2 * block_len, model_width)
    query_idx = lax.broadcasted_iota(jnp.int32, (block_len, 2 * block_len), 0)
    key_idx = lax.broadcasted_iota(jnp.int32, (block_len, 2 * block_len), 1)
    allowed = (key_idx <= query_idx + block_len) & ((key_idx >= block_len) | (device_idx > 0))
    hidden = embedded
    for layer_idx in range(LAYERS):
        hidden = attention_layer(
            hidden,
            w_qkv[layer_idx],
            w_out[layer_idx],
            w_pos[layer_idx],
            bias_content[layer_idx],
            bias_position[layer_idx],
            norm_gain[layer_idx],
            norm_offset[layer_idx],
            pos_table,
            allowed,
        )
    vocab_first = device_idx * table.shape[0]
    logits = jnp.einsum(
        "td,vd->tv",
        lax.all_gather(hidden, "seq", axis=0, tiled=True),
        table,
        preferred_element_type=jnp.float32,
    )
    exp_sums = jnp.sum(jnp.exp(logits), 1)
    wanted = targets - vocab_first
    columns = lax.broadcasted_iota(jnp.int32, logits.shape, 1)
    picked = jnp.sum(jnp.where(columns == wanted[:, None], logits, 0.0), 1)
    shard_stats = jnp.stack([exp_sums, picked])
    exp_sums, picked = (
        of_everyone(shard_stats[0].astype(jnp.bfloat16), "seq").astype(jnp.float32),
        of_everyone(shard_stats[1].astype(jnp.bfloat16), "seq").astype(jnp.float32),
    )
    doc_length = valid_length[0]
    token_idx = lax.broadcasted_iota(jnp.int32, exp_sums.shape, 0)
    per_token = jnp.where(token_idx < doc_length, jnp.log(exp_sums) - picked, 0.0)
    loss_value = (jnp.sum(per_token) / doc_length.astype(jnp.float32)).reshape(1)
    token_loss = lax.dynamic_slice_in_dim(per_token, device_idx * block_len, block_len)
    own_idx = device_idx * block_len + lax.broadcasted_iota(jnp.int32, (block_len, 1), 0)
    hidden_out = jnp.where(own_idx < doc_length, hidden, jnp.zeros_like(hidden))
    return (hidden_out, token_loss, loss_value)


def solution(mesh):
    in_specs = (
        P(("batch", "seq"), None),
        P(None, "seq", None),
        P(None, "seq", None),
        P(None, None, "seq"),
        P(),
        P(),
        P(),
        P(),
        P("seq", None),
        P("batch"),
        P("batch"),
    )
    out_specs = (P(("batch", "seq"), None), P(("batch", "seq")), P("batch"))
    return jax.shard_map(
        on_device, mesh=mesh, in_specs=in_specs, out_specs=out_specs, check_vma=False
    )
```

profile of v0, /device:TPU:6, one launch (start us, length us, event | category | flops | bytes accessed | tf_op | source)
XLA Modules:
  0.0 379.1 jit_solution(16822463815121106756)
XLA Ops:
  14.1 9.9 %all-to-all-start = ((bf16[32,256,32]{1,2,0:T(8,128)(2,1)}), bf16[32,256,32]{1,2,0:T(8,128)(2,1)S(1)}, u32[]{:S(2)}, u32[]{:S(2)}) async-start(bf16[32,256,32]{1,2,0:T(8,128)(2,1)} %broadcast_in_dim.86), calls=%async_computation | async-start | bytes 1048576 | tf_op jit(solution)/shard_map/all_to_all | solution.py:19
  24.3 23.0 %all-to-all-done = bf16[32,256,32]{1,2,0:T(8,128)(2,1)S(1)} async-done(((bf16[32,256,32]{1,2,0:T(8,128)(2,1)}), bf16[32,256,32]{1,2,0:T(8,128)(2,1)S(1)}, u32[]{:S(2)}, u32[]{:S(2)}) %all-to-all-start) | async-done | bytes 524320 | tf_op jit(solution)/shard_map/all_to_all | solution.py:19
  48.2 3.9 %all-to-all-start.2 = ((bf16[32,256,32]{1,2,0:T(8,128)(2,1)}), bf16[32,256,32]{1,2,0:T(8,128)(2,1)S(1)}, u32[]{:S(2)}, u32[]{:S(2)}) async-start(bf16[32,256,32]{1,2,0:T(8,128)(2,1)} %broadcast_in_dim.90), calls=%async_computation.2 | async-start | bytes 1048576 | tf_op jit(solution)/shard_map/all_to_all | solution.py:19
  52.1 21.8 %all-to-all-done.2 = bf16[32,256,32]{1,2,0:T(8,128)(2,1)S(1)} async-done(((bf16[32,256,32]{1,2,0:T(8,128)(2,1)}), bf16[32,256,32]{1,2,0:T(8,128)(2,1)S(1)}, u32[]{:S(2)}, u32[]{:S(2)}) %all-to-all-start.2) | async-done | bytes 524320 | tf_op jit(solution)/shard_map/all_to_all | solution.py:19
  75.5 5.2 %all-to-all-start.1 = ((bf16[32,32,1024]{2,1,0:T(8,128)(2,1)}), bf16[32,32,1024]{2,1,0:T(8,128)(2,1)}, u32[]{:S(2)}, u32[]{:S(2)}) async-start(bf16[32,32,1024]{2,1,0:T(8,128)(2,1)} %broadcast_in_dim.89), calls=%async_computation.1 | async-start | bytes 4194304 | tf_op jit(solution)/shard_map/all_to_all | solution.py:19
  84.5 26.3 %all-gather.8.cloned.1.call-done = bf16[1,1024,3072]{2,1,0:T(8,128)(2,1)} async-done(((bf16[1,32,3072]{2,1,0:T(8,128)(2,1)}), bf16[1,1024,3072]{2,1,0:T(8,128)(2,1)}) %all-gather.8.cloned.1.call-update) | async-done | bytes 6291472 | tf_op jit(solution)/shard_map/all_gather | solution.py:74
  110.8 3.9 %fusion.43 = (bf16[128,3072]{1,0:T(8,128)(2,1)S(1)}, f32[128,3072]{1,0:T(8,128)S(1)}) fusion(bf16[128,1024]{1,0:T(8,128)(2,1)S(1)} %copy-done.4, bf16[1,1024,3072]{2,1,0:T(8,128)(2,1)} %all-gather.8.cloned.1.call-done), kind=kOutput, calls=%fused_computation.85 | convolution fusion | flops 805699584 | bytes 8912896 | tf_op jit(solution)/shard_map/dot_general | solution.py:76
  124.5 2.9 reshape.161
  132.1 3.0 fusion.15
  139.1 33.5 %all-to-all-start.3 = ((bf16[32,32,1024]{2,1,0:T(8,128)(2,1)}), bf16[32,32,1024]{2,1,0:T(8,128)(2,1)}, u32[]{:S(2)}, u32[]{:S(2)}) async-start(bf16[32,32,1024]{2,1,0:T(8,128)(2,1)} %broadcast_in_dim.92), calls=%async_computation.3 | async-start | bytes 4194304 | tf_op jit(solution)/shard_map/all_to_all | solution.py:19
  172.8 2.9 convolution_convert_fusion.1
  178.2 2.9 collective-permute-start.1
  181.1 15.6 %all-gather.10.cloned.1.call-done = bf16[1,1024,3072]{2,1,0:T(8,128)(2,1)} async-done(((bf16[1,32,3072]{2,1,0:T(8,128)(2,1)}), bf16[1,1024,3072]{2,1,0:T(8,128)(2,1)}) %all-gather.10.cloned.1.call-update) | async-done | bytes 6291472 | tf_op jit(solution)/shard_map/all_gather | solution.py:74
  196.8 4.7 %fusion.45 = (bf16[128,3072]{1,0:T(8,128)(2,1)}, f32[128,3072]{1,0:T(8,128)S(1)}) fusion(bf16[128,1024]{1,0:T(8,128)(2,1)S(1)} %add_convert_fusion.3, bf16[1,1024,3072]{2,1,0:T(8,128)(2,1)} %all-gather.10.cloned.1.call-done), kind=kOutput, calls=%fused_computation.87 | convolution fusion | flops 805699584 | bytes 8912896 | tf_op jit(solution)/shard_map/dot_general | solution.py:76
  205.5 2.9 reshape.169
  212.1 3.0 fusion.7
  222.6 3.0 fusion.12
  225.7 2.9 convolution_convert_fusion
  232.1 86.8 %all-gather.6.cloned.1.call-done = bf16[4096,1024]{1,0:T(8,128)(2,1)} async-done(((bf16[128,1024]{1,0:T(8,128)(2,1)}), bf16[4096,1024]{1,0:T(8,128)(2,1)}) %all-gather.6.cloned.1.call-update) | async-done | bytes 8388624 | tf_op jit(solution)/shard_map/all_gather | solution.py:160
  319.0 9.8 %exponential_reduce_fusion = (bf16[4096]{0:T(1024)(128)(2,1)S(1)}, bf16[4096]{0:T(1024)(128)(2,1)S(1)}) fusion(s32[4096]{0:T(1024)S(1)} %broadcast_subtract_fusion, bf16[4096,1024]{1,0:T(8,128)(2,1)} %all-gather.6.cloned.1.call-done, bf16[384,1024]{1,0:T(8,128)(2,1)S(1)} %copy-done), kind=kOutput, calls=%fused_computation.2 | convolution fusion | flops 3227508736 | bytes 9207808 | tf_op jit(solution)/shard_map/td,vd->tv/dot_general | solution.py:158
  332.8 5.9 %all-to-all-start.5 = ((bf16[32,2,2048]{2,1,0:T(2,128)(2,1)}), bf16[32,2,2048]{2,1,0:T(2,128)(2,1)S(1)}, u32[]{:S(2)}, u32[]{:S(2)}) async-start(bf16[32,2,2048]{2,1,0:T(2,128)(2,1)} %reshape.176), calls=%async_computation.5 | async-start | bytes 524288 | tf_op jit(solution)/shard_map/all_to_all | solution.py:19
  342.2 9.6 %all-to-all-done.5 = bf16[32,2,2048]{2,1,0:T(2,128)(2,1)S(1)} async-done(((bf16[32,2,2048]{2,1,0:T(2,128)(2,1)}), bf16[32,2,2048]{2,1,0:T(2,128)(2,1)S(1)}, u32[]{:S(2)}, u32[]{:S(2)}) %all-to-all-start.5) | async-done | bytes 262176 | tf_op jit(solution)/shard_map/all_to_all | solution.py:19
  351.8 3.9 %all-to-all-start.4 = ((bf16[32,2,2048]{2,1,0:T(2,128)(2,1)}), bf16[32,2,2048]{2,1,0:T(2,128)(2,1)S(1)}, u32[]{:S(2)}, u32[]{:S(2)}) async-start(bf16[32,2,2048]{2,1,0:T(2,128)(2,1)} %reshape.178), calls=%async_computation.4 | async-start | bytes 524288 | tf_op jit(solution)/shard_map/all_to_all | solution.py:19
  356.3 12.5 %all-to-all-done.4 = bf16[32,2,2048]{2,1,0:T(2,128)(2,1)S(1)} async-done(((bf16[32,2,2048]{2,1,0:T(2,128)(2,1)}), bf16[32,2,2048]{2,1,0:T(2,128)(2,1)S(1)}, u32[]{:S(2)}, u32[]{:S(2)}) %all-to-all-start.4) | async-done | bytes 262176 | tf_op jit(solution)/shard_map/all_to_all | solution.py:19
  (108 shorter events, 62.4 us)
Async XLA Ops:
  7.2 311.8 %copy-start = (bf16[384,1024]{1,0:T(8,128)(2,1)S(1)}, bf16[384,1024]{1,0:T(8,128)(2,1)}, u32[]{:S(2)}) copy-start(bf16[384,1024]{1,0:T(8,128)(2,1)} %param.19) | copy-start | bytes 2359300
  7.2 16.8 %copy-start.13 = (bf16[2,1024,32]{1,2,0:T(8,128)(2,1)S(1)}, bf16[2,1024,32]{1,2,0:T(8,128)(2,1)}, u32[]{:S(2)}) copy-start(bf16[2,1024,32]{1,2,0:T(8,128)(2,1)} %param.14) | copy-start | bytes 393220
  7.2 103.6 %all-gather.8.cloned.1.call-start = ((), (), s32[]{:S(2)}) async-start(), calls=%async_computation.7 | async-start | bytes 6488064 | tf_op jit(solution)/shard_map/all_gather | solution.py:74
  9.1 187.7 %all-gather.10.cloned.1.call-start = ((), (), s32[]{:S(2)}) async-start(), calls=%async_computation.8 | async-start | bytes 6488064 | tf_op jit(solution)/shard_map/all_gather | solution.py:74
  13.2 38.9 %copy-start.7 = (bf16[2,32,1024]{2,1,0:T(8,128)(2,1)S(1)}, bf16[2,32,1024]{2,1,0:T(8,128)(2,1)}, u32[]{:S(2)}) copy-start(bf16[2,32,1024]{2,1,0:T(8,128)(2,1)} %param.13) | copy-start | bytes 393220
  14.1 33.1 %all-to-all-start = ((bf16[32,256,32]{1,2,0:T(8,128)(2,1)}), bf16[32,256,32]{1,2,0:T(8,128)(2,1)S(1)}, u32[]{:S(2)}, u32[]{:S(2)}) async-start(bf16[32,256,32]{1,2,0:T(8,128)(2,1)} %broadcast_in_dim.86), calls=%async_computation | async-start | bytes 1048576 | tf_op jit(solution)/shard_map/all_to_all | solution.py:19
  48.2 25.8 %all-to-all-start.2 = ((bf16[32,256,32]{1,2,0:T(8,128)(2,1)}), bf16[32,256,32]{1,2,0:T(8,128)(2,1)S(1)}, u32[]{:S(2)}, u32[]{:S(2)}) async-start(bf16[32,256,32]{1,2,0:T(8,128)(2,1)} %broadcast_in_dim.90), calls=%async_computation.2 | async-start | bytes 1048576 | tf_op jit(solution)/shard_map/all_to_all | solution.py:19
  75.5 5.3 %copy-start.4 = (bf16[128,1024]{1,0:T(8,128)(2,1)S(1)}, bf16[128,1024]{1,0:T(8,128)(2,1)}, u32[]{:S(2)}) copy-start(bf16[128,1024]{1,0:T(8,128)(2,1)} %param.11) | copy-start | bytes 786436
  75.5 8.8 %copy-start.9 = (f32[2,1024]{1,0:T(2,128)S(1)}, f32[2,1024]{1,0:T(2,128)}, u32[]{:S(2)}) copy-start(f32[2,1024]{1,0:T(2,128)} %param.15) | copy-start | bytes 24580
  75.5 8.8 %copy-start.10 = (f32[2,1024]{1,0:T(2,128)S(1)}, f32[2,1024]{1,0:T(2,128)}, u32[]{:S(2)}) copy-start(f32[2,1024]{1,0:T(2,128)} %param.16) | copy-start | bytes 24580
  75.5 8.9 %copy-start.11 = (f32[2,1024]{1,0:T(2,128)S(1)}, f32[2,1024]{1,0:T(2,128)}, u32[]{:S(2)}) copy-start(f32[2,1024]{1,0:T(2,128)} %param.17) | copy-start | bytes 24580
  75.5 8.9 %copy-start.12 = (f32[2,1024]{1,0:T(2,128)S(1)}, f32[2,1024]{1,0:T(2,128)}, u32[]{:S(2)}) copy-start(f32[2,1024]{1,0:T(2,128)} %param.18) | copy-start | bytes 24580
  75.5 61.9 %all-to-all-start.1 = ((bf16[32,32,1024]{2,1,0:T(8,128)(2,1)}), bf16[32,32,1024]{2,1,0:T(8,128)(2,1)}, u32[]{:S(2)}, u32[]{:S(2)}) async-start(bf16[32,32,1024]{2,1,0:T(8,128)(2,1)} %broadcast_in_dim.89), calls=%async_computation.1 | async-start | bytes 4194304 | tf_op jit(solution)/shard_map/all_to_all | solution.py:19
  80.8 34.0 %collective-permute-start = (bf16[128,1024]{1,0:T(8,128)(2,1)S(1)}, bf16[128,1024]{1,0:T(8,128)(2,1)}, u32[]{:S(2)}, u32[]{:S(2)}) collective-permute-start(bf16[128,1024]{1,0:T(8,128)(2,1)S(1)} %copy-done.4), channel_id=1, source_target_pairs={{0,8},{8,16},{16,24},{24,32},{32,40},{40,48},{48,56},{56,64},{64,7... | collective-permute-start | bytes 786440 | tf_op jit(solution)/shard_map/ppermute | solution.py:14
  110.8 4.6 %copy-start.1 = (bf16[1,1024,3072]{2,1,0:T(8,128)(2,1)S(1)}, bf16[1,1024,3072]{2,1,0:T(8,128)(2,1)}, u32[]{:S(2)}) copy-start(bf16[1,1024,3072]{2,1,0:T(8,128)(2,1)} %all-gather.8.cloned.1.call-done) | copy-start | bytes 18874372
  139.1 33.6 %copy-start.6 = (bf16[256,1024]{0,1:T(8,128)(2,1)S(1)}, bf16[256,1024]{0,1:T(8,128)(2,1)}, u32[]{:S(2)}) copy-start(bf16[256,1024]{0,1:T(8,128)(2,1)} %copy.48) | copy-start | bytes 1572868
  139.1 89.5 %all-to-all-start.3 = ((bf16[32,32,1024]{2,1,0:T(8,128)(2,1)}), bf16[32,32,1024]{2,1,0:T(8,128)(2,1)}, u32[]{:S(2)}, u32[]{:S(2)}) async-start(bf16[32,32,1024]{2,1,0:T(8,128)(2,1)} %broadcast_in_dim.92), calls=%async_computation.3 | async-start | bytes 4194304 | tf_op jit(solution)/shard_map/all_to_all | solution.py:19
  172.7 146.3 %all-gather.6.cloned.1.call-start = ((), (), s32[]{:S(2)}) async-start(), calls=%async_computation.6 | async-start | bytes 8650752 | tf_op jit(solution)/shard_map/all_gather | solution.py:160
  172.8 2.9 copy-start.5
  178.2 24.2 %copy-start.3 = (bf16[32,256,32]{1,2,0:T(8,128)(2,1)S(1)}, bf16[32,256,32]{1,2,0:T(8,128)(2,1)}, u32[]{:S(2)}) copy-start(bf16[32,256,32]{1,2,0:T(8,128)(2,1)} %copy-done.2) | copy-start | bytes 1572868
  178.2 33.9 %collective-permute-start.1 = (bf16[128,1024]{1,0:T(8,128)(2,1)S(1)}, bf16[128,1024]{1,0:T(8,128)(2,1)}, u32[]{:S(2)}, u32[]{:S(2)}) collective-permute-start(bf16[128,1024]{1,0:T(8,128)(2,1)S(1)} %add_convert_fusion.3), channel_id=1, source_target_pairs={{0,8},{8,16},{16,24},{24,32},{32,40},{40,48},{48,56},{56,64},{64,7... | collective-permute-start | bytes 786440 | tf_op jit(solution)/shard_map/ppermute | solution.py:14
  228.6 3.5 copy-start.8
  332.8 19.0 %all-to-all-start.5 = ((bf16[32,2,2048]{2,1,0:T(2,128)(2,1)}), bf16[32,2,2048]{2,1,0:T(2,128)(2,1)S(1)}, u32[]{:S(2)}, u32[]{:S(2)}) async-start(bf16[32,2,2048]{2,1,0:T(2,128)(2,1)} %reshape.176), calls=%async_computation.5 | async-start | bytes 524288 | tf_op jit(solution)/shard_map/all_to_all | solution.py:19
  351.8 17.0 %all-to-all-start.4 = ((bf16[32,2,2048]{2,1,0:T(2,128)(2,1)}), bf16[32,2,2048]{2,1,0:T(2,128)(2,1)S(1)}, u32[]{:S(2)}, u32[]{:S(2)}) async-start(bf16[32,2,2048]{2,1,0:T(2,128)(2,1)} %reshape.178), calls=%async_computation.4 | async-start | bytes 524288 | tf_op jit(solution)/shard_map/all_to_all | solution.py:19
  (1 other events, 1.6 us)
Sparse Core Ops, SparseCore 0:
  10.4 100.3 all-gather.7
  112.7 84.0 all-gather.9
  232.2 86.6 all-gather.5
where the time goes:
time: 380 us; the launch traced here: 379 us
  waiting for transfers between devices  199 us (52%)
  starting transfers between devices  68.1 us (18%)
  matrix products  41.5 us (11%)
  local copies, waits for them, and re-layouts  38.7 us (10%)
  between operations  16.8 us (4%)
  other arithmetic  15.1 us (4%)
    all_gather x1, waiting for transfers between devices, on_device(): lax.all_gather(hidden, 'seq', axis=0, tiled=True)  86.8 us
    all_to_all x6, waiting for transfers between devices, copy_for_each(): lax.all_to_all(jnp.broadcast_to(x[None], (devices, *x.shape)), axis, 0, 0...  69.3 us
    all_to_all x6, starting transfers between devices, copy_for_each(): lax.all_to_all(jnp.broadcast_to(x[None], (devices, *x.shape)), axis, 0, 0...  62.2 us
    all_gather x2, waiting for transfers between devices, attention_layer(): piece_rows = lax.all_gather(qkv_shard, 'seq', axis=0, tiled=True)  42 us
    dot_general x1, matrix products, on_device(): jnp.einsum('td,vd->tv', lax.all_gather(hidden, 'seq', axis=0, tiled=True)...  9.81 us
    dot_general x2, matrix products, attention_layer(): own_part = jnp.dot(own_cols, piece_rows, preferred_element_type=jnp.float32)  8.62 us
  transfers between devices with their start and end apart: 11, of which 8 were waited for; matrix products, arithmetic and copies ran while one was open for 19% of the time, Pallas kernels for 0%

commit v1 on v0

--- a/solution.py
+++ b/solution.py
@@ -157,7 +157,9 @@
     vocab_first = device_idx * table.shape[0]
     logits = jnp.einsum(
         "td,vd->tv",
-        lax.all_gather(hidden, "seq", axis=0, tiled=True),
+        jnp.concatenate(
+            lax.all_to_all(jnp.stack([hidden] * lax.axis_size("seq")), "seq", 0, 0), axis=0
+        ),
         table,
         preferred_element_type=jnp.float32,
     )

time: 380 us -> 508 us (1.34)
  waiting for transfers between devices: 199 us -> 298 us
  starting transfers between devices: 68.1 us -> 92.4 us
    all_to_all x0 -> x1, waiting for transfers between devices: none -> 186 us  [on_device(): lax.all_to_all(jnp.stack([hidden] * lax.axis_size('seq')), 'seq', 0, 0)]
    all_gather x1 -> x0, waiting for transfers between devices: 86.8 us -> none  [on_device(): lax.all_gather(hidden, 'seq', axis=0, tiled=True)]
    all_to_all x0 -> x1, starting transfers between devices: none -> 21.8 us  [on_device(): lax.all_to_all(jnp.stack([hidden] * lax.axis_size('seq')), 'seq', 0, 0)]
  transfers between devices with their start and end apart: 11 -> 11, of which waited for: 8 -> 8; matrix products, arithmetic and copies ran while one was open for 19% -> 15% of each run, Pallas kernels for 0% -> 0%
where the time goes in v1:
time: 508 us; the launch traced here: 507 us
  waiting for transfers between devices  298 us (59%)
  starting transfers between devices  92.4 us (18%)
  local copies, waits for them, and re-layouts  43 us (8%)
  matrix products  41.6 us (8%)
  between operations  17.1 us (3%)
  other arithmetic  15 us (3%)
    all_to_all x1, waiting for transfers between devices, on_device(): lax.all_to_all(jnp.stack([hidden] * lax.axis_size('seq')), 'seq', 0, 0)  186 us
    all_to_all x6, waiting for transfers between devices, copy_for_each(): lax.all_to_all(jnp.broadcast_to(x[None], (devices, *x.shape)), axis, 0, 0...  68.4 us
    all_to_all x6, starting transfers between devices, copy_for_each(): lax.all_to_all(jnp.broadcast_to(x[None], (devices, *x.shape)), axis, 0, 0...  64.7 us
    all_gather x2, waiting for transfers between devices, attention_layer(): piece_rows = lax.all_gather(qkv_shard, 'seq', axis=0, tiled=True)  42.8 us
    all_to_all x1, starting transfers between devices, on_device(): lax.all_to_all(jnp.stack([hidden] * lax.axis_size('seq')), 'seq', 0, 0)  21.8 us
  transfers between devices with their start and end apart: 11, of which 8 were waited for; matrix products, arithmetic and copies ran while one was open for 15% of the time, Pallas kernels for 0%

profile of v1, /device:TPU:6, one launch (start us, length us, event | category | flops | bytes accessed | tf_op | source)
XLA Modules:
  0.0 506.9 jit_solution(4792951667401832167)
XLA Ops:
  14.1 9.9 %all-to-all-start = ((bf16[32,256,32]{1,2,0:T(8,128)(2,1)}), bf16[32,256,32]{1,2,0:T(8,128)(2,1)S(1)}, u32[]{:S(2)}, u32[]{:S(2)}) async-start(bf16[32,256,32]{1,2,0:T(8,128)(2,1)} %broadcast_in_dim.86), calls=%async_computation | async-start | bytes 1048576 | tf_op jit(solution)/shard_map/all_to_all | solution.py:19
  24.3 23.0 %all-to-all-done = bf16[32,256,32]{1,2,0:T(8,128)(2,1)S(1)} async-done(((bf16[32,256,32]{1,2,0:T(8,128)(2,1)}), bf16[32,256,32]{1,2,0:T(8,128)(2,1)S(1)}, u32[]{:S(2)}, u32[]{:S(2)}) %all-to-all-start) | async-done | bytes 524320 | tf_op jit(solution)/shard_map/all_to_all | solution.py:19
  48.2 3.9 all-to-all-start.2
  52.1 21.8 %all-to-all-done.2 = bf16[32,256,32]{1,2,0:T(8,128)(2,1)S(1)} async-done(((bf16[32,256,32]{1,2,0:T(8,128)(2,1)}), bf16[32,256,32]{1,2,0:T(8,128)(2,1)S(1)}, u32[]{:S(2)}, u32[]{:S(2)}) %all-to-all-start.2) | async-done | bytes 524320 | tf_op jit(solution)/shard_map/all_to_all | solution.py:19
  75.5 5.3 %all-to-all-start.1 = ((bf16[32,32,1024]{2,1,0:T(8,128)(2,1)}), bf16[32,32,1024]{2,1,0:T(8,128)(2,1)}, u32[]{:S(2)}, u32[]{:S(2)}) async-start(bf16[32,32,1024]{2,1,0:T(8,128)(2,1)} %broadcast_in_dim.89), calls=%async_computation.1 | async-start | bytes 4194304 | tf_op jit(solution)/shard_map/all_to_all | solution.py:19
  84.5 26.9 %all-gather.5.cloned.1.call-done = bf16[1,1024,3072]{2,1,0:T(8,128)(2,1)} async-done(((bf16[1,32,3072]{2,1,0:T(8,128)(2,1)}), bf16[1,1024,3072]{2,1,0:T(8,128)(2,1)}) %all-gather.5.cloned.1.call-update) | async-done | bytes 6291472 | tf_op jit(solution)/shard_map/all_gather | solution.py:74
  111.4 3.9 fusion.43
  125.1 2.9 reshape.166
  132.7 3.0 fusion.15
  138.9 33.8 %all-to-all-start.3 = ((bf16[32,32,1024]{2,1,0:T(8,128)(2,1)}), bf16[32,32,1024]{2,1,0:T(8,128)(2,1)}, u32[]{:S(2)}, u32[]{:S(2)}) async-start(bf16[32,32,1024]{2,1,0:T(8,128)(2,1)} %broadcast_in_dim.92), calls=%async_computation.3 | async-start | bytes 4194304 | tf_op jit(solution)/shard_map/all_to_all | solution.py:19
  178.2 3.0 collective-permute-start.1
  181.1 15.9 %all-gather.7.cloned.1.call-done = bf16[1,1024,3072]{2,1,0:T(8,128)(2,1)} async-done(((bf16[1,32,3072]{2,1,0:T(8,128)(2,1)}), bf16[1,1024,3072]{2,1,0:T(8,128)(2,1)}) %all-gather.7.cloned.1.call-update) | async-done | bytes 6291472 | tf_op jit(solution)/shard_map/all_gather | solution.py:74
  197.0 4.7 fusion.45
  212.4 3.0 fusion.7
  222.9 3.0 fusion.12
  225.9 2.9 convolution_convert_fusion
  232.2 4.3 stack.2
  236.6 21.8 %all-to-all-start.4 = ((bf16[32,128,1024]{2,1,0:T(8,128)(2,1)}), bf16[32,128,1024]{2,1,0:T(8,128)(2,1)}, u32[]{:S(2)}, u32[]{:S(2)}) async-start(bf16[32,128,1024]{2,1,0:T(8,128)(2,1)} %stack.2), calls=%async_computation.4 | async-start | bytes 16777216 | tf_op jit(solution)/shard_map/all_to_all | solution.py:161
  258.4 185.9 %all-to-all-done.4 = bf16[32,128,1024]{2,1,0:T(8,128)(2,1)} async-done(((bf16[32,128,1024]{2,1,0:T(8,128)(2,1)}), bf16[32,128,1024]{2,1,0:T(8,128)(2,1)}, u32[]{:S(2)}, u32[]{:S(2)}) %all-to-all-start.4) | async-done | bytes 8388640 | tf_op jit(solution)/shard_map/all_to_all | solution.py:161
  444.3 9.8 %exponential_reduce_fusion = (bf16[4096]{0:T(1024)(128)(2,1)S(1)}, bf16[4096]{0:T(1024)(128)(2,1)S(1)}) fusion(s32[4096]{0:T(1024)S(1)} %broadcast_subtract_fusion, bf16[4096,1024]{1,0:T(8,128)(2,1)} %bitcast.33, bf16[384,1024]{1,0:T(8,128)(2,1)S(1)} %copy-done), kind=kOutput, calls=%fused_computation.2 | convolution fusion | flops 3227508736 | bytes 9207808 | tf_op jit(solution)/shard_map/td,vd->tv/dot_general | solution.py:158
  458.2 8.0 %all-to-all-start.6 = ((bf16[32,2,2048]{2,1,0:T(2,128)(2,1)}), bf16[32,2,2048]{2,1,0:T(2,128)(2,1)S(1)}, u32[]{:S(2)}, u32[]{:S(2)}) async-start(bf16[32,2,2048]{2,1,0:T(2,128)(2,1)} %reshape.182), calls=%async_computation.6 | async-start | bytes 524288 | tf_op jit(solution)/shard_map/all_to_all | solution.py:19
  469.7 9.6 %all-to-all-done.6 = bf16[32,2,2048]{2,1,0:T(2,128)(2,1)S(1)} async-done(((bf16[32,2,2048]{2,1,0:T(2,128)(2,1)}), bf16[32,2,2048]{2,1,0:T(2,128)(2,1)S(1)}, u32[]{:S(2)}, u32[]{:S(2)}) %all-to-all-start.6) | async-done | bytes 262176 | tf_op jit(solution)/shard_map/all_to_all | solution.py:19
  479.3 3.9 all-to-all-start.5
  483.8 12.5 %all-to-all-done.5 = bf16[32,2,2048]{2,1,0:T(2,128)(2,1)S(1)} async-done(((bf16[32,2,2048]{2,1,0:T(2,128)(2,1)}), bf16[32,2,2048]{2,1,0:T(2,128)(2,1)S(1)}, u32[]{:S(2)}, u32[]{:S(2)}) %all-to-all-start.5) | async-done | bytes 262176 | tf_op jit(solution)/shard_map/all_to_all | solution.py:19
  (108 shorter events, 67.1 us)
Async XLA Ops:
  7.2 437.1 %copy-start = (bf16[384,1024]{1,0:T(8,128)(2,1)S(1)}, bf16[384,1024]{1,0:T(8,128)(2,1)}, u32[]{:S(2)}) copy-start(bf16[384,1024]{1,0:T(8,128)(2,1)} %param.19) | copy-start | bytes 2359300
  7.2 16.8 %copy-start.13 = (bf16[2,1024,32]{1,2,0:T(8,128)(2,1)S(1)}, bf16[2,1024,32]{1,2,0:T(8,128)(2,1)}, u32[]{:S(2)}) copy-start(bf16[2,1024,32]{1,2,0:T(8,128)(2,1)} %param.14) | copy-start | bytes 393220
  7.2 104.2 %all-gather.5.cloned.1.call-start = ((), (), s32[]{:S(2)}) async-start(), calls=%async_computation.7 | async-start | bytes 6488064 | tf_op jit(solution)/shard_map/all_gather | solution.py:74
  9.1 187.9 %all-gather.7.cloned.1.call-start = ((), (), s32[]{:S(2)}) async-start(), calls=%async_computation.8 | async-start | bytes 6488064 | tf_op jit(solution)/shard_map/all_gather | solution.py:74
  13.2 38.8 %copy-start.7 = (bf16[2,32,1024]{2,1,0:T(8,128)(2,1)S(1)}, bf16[2,32,1024]{2,1,0:T(8,128)(2,1)}, u32[]{:S(2)}) copy-start(bf16[2,32,1024]{2,1,0:T(8,128)(2,1)} %param.13) | copy-start | bytes 393220
  14.1 33.1 %all-to-all-start = ((bf16[32,256,32]{1,2,0:T(8,128)(2,1)}), bf16[32,256,32]{1,2,0:T(8,128)(2,1)S(1)}, u32[]{:S(2)}, u32[]{:S(2)}) async-start(bf16[32,256,32]{1,2,0:T(8,128)(2,1)} %broadcast_in_dim.86), calls=%async_computation | async-start | bytes 1048576 | tf_op jit(solution)/shard_map/all_to_all | solution.py:19
  48.2 25.7 %all-to-all-start.2 = ((bf16[32,256,32]{1,2,0:T(8,128)(2,1)}), bf16[32,256,32]{1,2,0:T(8,128)(2,1)S(1)}, u32[]{:S(2)}, u32[]{:S(2)}) async-start(bf16[32,256,32]{1,2,0:T(8,128)(2,1)} %broadcast_in_dim.90), calls=%async_computation.2 | async-start | bytes 1048576 | tf_op jit(solution)/shard_map/all_to_all | solution.py:19
  75.4 5.3 %copy-start.4 = (bf16[128,1024]{1,0:T(8,128)(2,1)S(1)}, bf16[128,1024]{1,0:T(8,128)(2,1)}, u32[]{:S(2)}) copy-start(bf16[128,1024]{1,0:T(8,128)(2,1)} %param.11) | copy-start | bytes 786436
  75.4 8.9 %copy-start.9 = (f32[2,1024]{1,0:T(2,128)S(1)}, f32[2,1024]{1,0:T(2,128)}, u32[]{:S(2)}) copy-start(f32[2,1024]{1,0:T(2,128)} %param.15) | copy-start | bytes 24580
  75.4 8.9 %copy-start.10 = (f32[2,1024]{1,0:T(2,128)S(1)}, f32[2,1024]{1,0:T(2,128)}, u32[]{:S(2)}) copy-start(f32[2,1024]{1,0:T(2,128)} %param.16) | copy-start | bytes 24580
  75.4 8.9 %copy-start.11 = (f32[2,1024]{1,0:T(2,128)S(1)}, f32[2,1024]{1,0:T(2,128)}, u32[]{:S(2)}) copy-start(f32[2,1024]{1,0:T(2,128)} %param.17) | copy-start | bytes 24580
  75.4 8.9 %copy-start.12 = (f32[2,1024]{1,0:T(2,128)S(1)}, f32[2,1024]{1,0:T(2,128)}, u32[]{:S(2)}) copy-start(f32[2,1024]{1,0:T(2,128)} %param.18) | copy-start | bytes 24580
  75.5 61.7 %all-to-all-start.1 = ((bf16[32,32,1024]{2,1,0:T(8,128)(2,1)}), bf16[32,32,1024]{2,1,0:T(8,128)(2,1)}, u32[]{:S(2)}, u32[]{:S(2)}) async-start(bf16[32,32,1024]{2,1,0:T(8,128)(2,1)} %broadcast_in_dim.89), calls=%async_computation.1 | async-start | bytes 4194304 | tf_op jit(solution)/shard_map/all_to_all | solution.py:19
  80.8 34.6 %collective-permute-start = (bf16[128,1024]{1,0:T(8,128)(2,1)S(1)}, bf16[128,1024]{1,0:T(8,128)(2,1)}, u32[]{:S(2)}, u32[]{:S(2)}) collective-permute-start(bf16[128,1024]{1,0:T(8,128)(2,1)S(1)} %copy-done.4), channel_id=1, source_target_pairs={{0,8},{8,16},{16,24},{24,32},{32,40},{40,48},{48,56},{56,64},{64,7... | collective-permute-start | bytes 786440 | tf_op jit(solution)/shard_map/ppermute | solution.py:14
  111.4 4.6 copy-start.1
  138.8 33.8 %copy-start.6 = (bf16[256,1024]{0,1:T(8,128)(2,1)S(1)}, bf16[256,1024]{0,1:T(8,128)(2,1)}, u32[]{:S(2)}) copy-start(bf16[256,1024]{0,1:T(8,128)(2,1)} %copy.48) | copy-start | bytes 1572868
  138.9 90.0 %all-to-all-start.3 = ((bf16[32,32,1024]{2,1,0:T(8,128)(2,1)}), bf16[32,32,1024]{2,1,0:T(8,128)(2,1)}, u32[]{:S(2)}, u32[]{:S(2)}) async-start(bf16[32,32,1024]{2,1,0:T(8,128)(2,1)} %broadcast_in_dim.92), calls=%async_computation.3 | async-start | bytes 4194304 | tf_op jit(solution)/shard_map/all_to_all | solution.py:19
  172.7 2.9 copy-start.5
  178.2 24.5 %copy-start.3 = (bf16[32,256,32]{1,2,0:T(8,128)(2,1)S(1)}, bf16[32,256,32]{1,2,0:T(8,128)(2,1)}, u32[]{:S(2)}) copy-start(bf16[32,256,32]{1,2,0:T(8,128)(2,1)} %copy-done.2) | copy-start | bytes 1572868
  178.2 34.2 %collective-permute-start.1 = (bf16[128,1024]{1,0:T(8,128)(2,1)S(1)}, bf16[128,1024]{1,0:T(8,128)(2,1)}, u32[]{:S(2)}, u32[]{:S(2)}) collective-permute-start(bf16[128,1024]{1,0:T(8,128)(2,1)S(1)} %add_convert_fusion.3), channel_id=1, source_target_pairs={{0,8},{8,16},{16,24},{24,32},{32,40},{40,48},{48,56},{56,64},{64,7... | collective-permute-start | bytes 786440 | tf_op jit(solution)/shard_map/ppermute | solution.py:14
  236.6 21.8 %copy-start.8 = (s32[4096]{0:T(1024)S(1)}, s32[4096]{0:T(1024)}, u32[]{:S(2)}) copy-start(s32[4096]{0:T(1024)} %param.20) | copy-start | bytes 49156
  236.6 207.7 %all-to-all-start.4 = ((bf16[32,128,1024]{2,1,0:T(8,128)(2,1)}), bf16[32,128,1024]{2,1,0:T(8,128)(2,1)}, u32[]{:S(2)}, u32[]{:S(2)}) async-start(bf16[32,128,1024]{2,1,0:T(8,128)(2,1)} %stack.2), calls=%async_computation.4 | async-start | bytes 16777216 | tf_op jit(solution)/shard_map/all_to_all | solution.py:161
  458.2 21.2 %all-to-all-start.6 = ((bf16[32,2,2048]{2,1,0:T(2,128)(2,1)}), bf16[32,2,2048]{2,1,0:T(2,128)(2,1)S(1)}, u32[]{:S(2)}, u32[]{:S(2)}) async-start(bf16[32,2,2048]{2,1,0:T(2,128)(2,1)} %reshape.182), calls=%async_computation.6 | async-start | bytes 524288 | tf_op jit(solution)/shard_map/all_to_all | solution.py:19
  479.3 17.0 %all-to-all-start.5 = ((bf16[32,2,2048]{2,1,0:T(2,128)(2,1)}), bf16[32,2,2048]{2,1,0:T(2,128)(2,1)S(1)}, u32[]{:S(2)}, u32[]{:S(2)}) async-start(bf16[32,2,2048]{2,1,0:T(2,128)(2,1)} %reshape.184), calls=%async_computation.5 | async-start | bytes 524288 | tf_op jit(solution)/shard_map/all_to_all | solution.py:19
  (1 other events, 1.6 us)
Sparse Core Ops, SparseCore 0:
  10.4 100.8 all-gather.4
  113.2 83.7 all-gather.6
